TPU v7x, 32 devices: a whole 2x2x4 slice. The times are simulated.
32 devices in a mesh: dp: 4 (over x, core), expert: 8 (over z, y).
Axes of the slice: x: 2, y: 2, z: 4, core: 2. Of those that a mesh axis runs over, the one named last changes fastest.
Arguments:
- queries: bfloat16 [2, 4, 8, 2048], P(None, 'dp', 'expert'), may hold values from -5 to 5
- cache_keys: bfloat16 [4, 8, 512, 512], P('dp', 'expert'), may hold values from -5 to 5
- cache_values: bfloat16 [4, 8, 512, 512], P('dp', 'expert'), may hold values from -6 to 6
- new_keys: bfloat16 [2, 4, 8, 512], P(None, 'dp', 'expert'), may hold values from -9 to 9
- new_values: bfloat16 [2, 4, 8, 512], P(None, 'dp', 'expert'), may hold values from -6 to 6
- cache_len: int32 [4, 8], P('dp', 'expert'), may hold values from 256 to 510, as said below
- o_proj: bfloat16 [2048, 4096], P(None, 'expert'), may hold values from -0.125 to 0.125
- residual_in: bfloat16 [2, 4, 8, 4096], P(None, 'dp', None, 'expert'), may hold values from -36 to 36
- norm_gain: float32 [4096], P('expert'), may hold values from 0.1 to 1.9
- router: float32 [4096, 8], P('expert'), may hold values from -0.09375 to 0.09375
- expert_gate: bfloat16 [8, 4096, 14336], P('expert', None, 'dp'), may hold values from -0.09375 to 0.09375
- expert_up: bfloat16 [8, 4096, 14336], P('expert', None, 'dp'), may hold values from -0.09375 to 0.09375
- expert_down: bfloat16 [8, 14336, 4096], P('expert', 'dp'), may hold values from -0.046875 to 0.046875
- routes: int32 [2, 4, 8, 2], replicated, may hold values from 0 to 7, all different within a row; in each aligned block of 8 rows (0 to 7, 8 to 15, ..., all dimensions but the last counted through in order) at most 4 rows name the same one
- answers: int32 [2, 4, 8], P(None, 'dp', 'expert'), may hold values from 0 to 127
- stop_mask: int32 [2, 4], P(None, 'dp'), may hold values 0 or 1
Outputs:
- residual_out: bfloat16 [2, 4, 8, 4096], P(None, 'dp', None, 'expert')
- vote_share: float32 [2, 4, 128], P(None, 'dp')
Inputs may be any that keep to these rules, and one draw needn't show every extreme that they name: `cache_len`: some sequence uses exactly 510 cached positions. `routes`: each token names 2 different experts; in each step, the tokens of the 1 prompts of one index of dp (all their samples together) name one expert at most 4 times.
All inputs are finite; a program needn't handle non-finite values. No bound on the sum of `stop_mask` on one device may be relied on, other than what follows from the above.
Results may differ from a plain program's by a relative error of at most 0.0055.
Values may be sent and summed in bfloat16 or wider, within the bound.
No kernel may reach another device: no remote copies, remote signals or barrier semaphores. Data moves between devices by JAX's collectives and lax.ppermute only.
A program may use at most 192 MiB of HBM per device.

v0:
```python
import jax
import jax.numpy as jnp
from jax import lax
from jax.sharding import PartitionSpec as P

D = 4096
E = 8
TOP = 2
HD = 128
QH = 16
KVH = 4
STEPS = 2
ANSWERS = 128
EPSILON = 1e-05


def attend(query, keys, values, fresh_keys, fresh_values, lengths):
    step_count = query.shape[0]
    row_count = query.shape[1]
    cache_size = keys.shape[1]
    group_size = QH // KVH
    score_scale = HD ** (-0.5)
    queried = query.reshape(step_count, row_count, KVH, group_size, HD)
    old_keys = keys.reshape(row_count, cache_size, KVH, HD)
    old_values = values.reshape(row_count, cache_size, KVH, HD)
    young_keys = fresh_keys.reshape(step_count, row_count, KVH, HD)
    young_values = fresh_values.reshape(step_count, row_count, KVH, HD)
    old_scores = (
        jnp.einsum("trkgd,rckd->rkgtc", queried, old_keys, preferred_element_type=jnp.float32)
        * score_scale
    )
    new_scores = (
        jnp.einsum("trkgd,urkd->rkgtu", queried, young_keys, preferred_element_type=jnp.float32)
        * score_scale
    )
    old_valid = jnp.arange(cache_size, dtype=jnp.int32)[None, :] < lengths[:, None]
    old_scores = jnp.where(old_valid[:, None, None, None, :], old_scores, -jnp.inf)
    new_valid = jnp.arange(step_count)[None, :] <= jnp.arange(step_count)[:, None]
    new_scores = jnp.where(new_valid, new_scores, -jnp.inf)
    highest = jnp.maximum(jnp.max(old_scores, -1), jnp.max(new_scores, -1))[..., None]
    old_exp = jnp.exp(old_scores - highest)
    new_exp = jnp.exp(new_scores - highest)
    denominator = jnp.sum(old_exp, -1, keepdims=True) + jnp.sum(new_exp, -1, keepdims=True)
    old_weights = (old_exp / denominator).astype(jnp.bfloat16)
    new_weights = (new_exp / denominator).astype(jnp.bfloat16)
    combined = jnp.einsum(
        "rkgtc,rckd->trkgd", old_weights, old_values, preferred_element_type=jnp.float32
    )
    combined = combined + jnp.einsum(
        "rkgtu,urkd->trkgd", new_weights, young_values, preferred_element_type=jnp.float32
    )
    return combined.reshape(step_count, row_count, QH * HD).astype(jnp.bfloat16)


def slot_tables(picks, capacity):
    block_count = picks.shape[0]
    row_count = picks.shape[1]
    expert_hot = (picks[..., None] == jnp.arange(E, dtype=jnp.int32)).astype(jnp.int32)
    expert_hot = expert_hot.reshape(block_count, row_count * TOP, E)
    earlier = jnp.cumsum(expert_hot, 1) - expert_hot
    place = jnp.sum(earlier * expert_hot, -1).reshape(block_count, row_count, TOP)
    slot_ids = picks * capacity + place
    return (slot_ids[..., None] == jnp.arange(E * capacity, dtype=jnp.int32)).astype(jnp.float32)


def on_device(
    queries,
    cache_keys,
    cache_values,
    new_keys,
    new_values,
    cache_len,
    o_proj,
    residual_in,
    norm_gain,
    router,
    expert_gate,
    expert_up,
    expert_down,
    routes,
    answers,
    stop_mask,
):
    prompt_dev = residual_in.shape[1]
    samples = residual_in.shape[2]
    columns = residual_in.shape[3]
    local_count = queries.shape[2]
    seq_count = prompt_dev * local_count
    cache_size = cache_keys.shape[2]
    spread = lax.axis_size("expert") // E
    capacity = 2 * prompt_dev * samples * TOP // E
    block_rows = prompt_dev * samples
    dp_index = lax.axis_index("dp")
    attended = attend(
        queries.reshape(STEPS, seq_count, QH * HD),
        cache_keys.reshape(seq_count, cache_size, KVH * HD),
        cache_values.reshape(seq_count, cache_size, KVH * HD),
        new_keys.reshape(STEPS, seq_count, KVH * HD),
        new_values.reshape(STEPS, seq_count, KVH * HD),
        cache_len.reshape(seq_count),
    ).reshape(STEPS, prompt_dev, local_count, QH * HD)
    active = (1 - stop_mask).astype(jnp.float32)
    attn_proj = jnp.einsum(
        "tpsq,qc->tpsc",
        lax.all_gather(attended, "expert", axis=2, tiled=True),
        o_proj,
        preferred_element_type=jnp.float32,
    )
    mixed_rows = residual_in.astype(jnp.float32) + attn_proj
    squares = jnp.sum(mixed_rows * mixed_rows, -1)
    scaled = mixed_rows * norm_gain
    squares_all = lax.psum(squares, "expert")
    inv_rms = lax.rsqrt(squares_all / D + EPSILON)[..., None]
    normed_f = scaled * inv_rms
    partial_logits = jnp.einsum("tpsc,ce->tpse", normed_f, router, precision=lax.Precision.HIGHEST)
    logits = lax.psum(partial_logits, "expert")
    normed = normed_f.astype(jnp.bfloat16)
    own_picks = lax.dynamic_slice_in_dim(routes, dp_index * prompt_dev, prompt_dev, 1)
    expert_hot = (own_picks[..., None] == jnp.arange(E, dtype=jnp.int32)).astype(jnp.float32)
    chosen = jnp.sum(expert_hot * logits[:, :, :, None, :], -1)
    gate_weights = jax.nn.sigmoid(chosen - chosen[..., ::-1]).reshape(STEPS, block_rows, TOP)
    own_table = slot_tables(own_picks.reshape(STEPS, block_rows, TOP), capacity)
    senders = jnp.sum(own_table, 2).astype(jnp.bfloat16)
    outgoing = jnp.einsum(
        "trs,trx->tsx",
        senders,
        normed.reshape(STEPS, block_rows, columns),
        preferred_element_type=jnp.float32,
    ).astype(jnp.bfloat16)
    outgoing = jnp.transpose(outgoing.reshape(STEPS, E, capacity, columns), (1, 0, 2, 3)).reshape(
        E, 1, STEPS * capacity, columns
    )
    outgoing = jnp.broadcast_to(outgoing, (E, spread, STEPS * capacity, columns)).reshape(
        E * spread, STEPS * capacity, columns
    )
    tokens = lax.all_gather(
        lax.all_to_all(outgoing, "expert", split_axis=0, concat_axis=2, tiled=True),
        "dp",
        axis=0,
        tiled=True,
    )
    gate_part = jnp.einsum(
        "...d,df->...f", tokens, expert_gate[0], preferred_element_type=jnp.float32
    )
    up_part = jnp.einsum("...d,df->...f", tokens, expert_up[0], preferred_element_type=jnp.float32)
    hidden = (jax.nn.silu(gate_part) * up_part).astype(jnp.bfloat16)
    partial_out = lax.psum_scatter(
        jnp.einsum("...f,fd->...d", hidden, expert_down[0], preferred_element_type=jnp.float32),
        "dp",
        scatter_dimension=0,
        tiled=True,
    )
    returned = lax.all_to_all(partial_out, "expert", split_axis=2, concat_axis=0, tiled=True)
    slot_out = jnp.sum(returned.reshape(E, spread, STEPS, capacity, columns), 1)
    slot_out = jnp.transpose(slot_out, (1, 0, 2, 3)).reshape(STEPS, E * capacity, columns)
    combine = jnp.einsum("trk,trks->trs", gate_weights, own_table)
    moe = jnp.einsum("trs,tsx->trx", combine, slot_out, precision=lax.Precision.HIGHEST).reshape(
        STEPS, prompt_dev, samples, columns
    )
    updated = residual_in.astype(jnp.float32) + active[:, :, None, None] * (attn_proj + moe)
    hits = jnp.sum(
        (answers[..., None] == jnp.arange(ANSWERS, dtype=jnp.int32)).astype(jnp.float32), 2
    )
    votes = active[:, :, None] * hits
    tallied = lax.psum(votes, "expert")
    running = jnp.cumsum(tallied, 0)
    shares = running / jnp.maximum(jnp.sum(running, -1, keepdims=True), 1.0)
    return (updated.astype(jnp.bfloat16), shares)


def solution(mesh):
    placed = (
        P(None, "dp", "expert", None),
        P("dp", "expert", None, None),
        P("dp", "expert", None, None),
        P(None, "dp", "expert", None),
        P(None, "dp", "expert", None),
        P("dp", "expert"),
        P(None, "expert"),
        P(None, "dp", None, "expert"),
        P("expert"),
        P("expert", None),
        P("expert", None, "dp"),
        P("expert", None, "dp"),
        P("expert", "dp", None),
        P(),
        P(None, "dp", "expert"),
        P(None, "dp"),
    )
    return jax.shard_map(
        on_device,
        mesh=mesh,
        in_specs=placed,
        out_specs=(P(None, "dp", None, "expert"), P(None, "dp", None)),
        check_vma=False,
    )
```

profile of v0, /device:TPU:0, one launch (start us, length us, event | category | flops | bytes accessed | tf_op | source)
XLA Modules:
  0.0 199.6 jit_solution(14043567168421434307)
XLA Ops:
  7.2 0.9 reshape.296
  8.1 1.2 reshape.295
  9.9 0.9 convolution_multiply_fusion.1
  11.6 1.2 reshape.299
  13.0 0.9 fusion.25
  13.9 32.4 %all_gather.6 = bf16[2,1,8,2048]{3,0,1,2:T(2,128)(2,1)S(1)} all-gather(bf16[2,1,1,2048]{3,0,1,2:T(2,128)(2,1)S(1)} %bitcast.171), channel_id=1, replica_groups=mesh['dp'=4,'expert'=8] {'expert'}, dimensions={2}, use_global_device_ids=true | all-gather | bytes 73728 | tf_op jit(solution)/shard_map/all_gather | solution.py:105
  46.3 1.2 multiply_reduce_fusion
  47.4 21.3 %psum.21 = f32[2,1,8]{2,0,1:T(2,128)S(1)} all-reduce(f32[2,1,8]{2,0,1:T(2,128)S(1)} %bitcast.173), channel_id=1, replica_groups=mesh['dp'=4,'expert'=8] {'expert'}, use_global_device_ids=true, to_apply=%region_5.6 | all-reduce | flops 16 | bytes 128 | tf_op jit(solution)/shard_map/psum | solution.py:112
  70.9 0.9 convolution_convert_fusion
  72.5 3.3 %all-to-all-start = ((bf16[8,8,512]{2,1,0:T(8,128)(2,1)}), bf16[8,8,512]{2,1,0:T(8,128)(2,1)S(1)}, u32[]{:S(2)}, u32[]{:S(2)}) async-start(bf16[8,8,512]{2,1,0:T(8,128)(2,1)} %copy.113), calls=%async_computation | async-start | bytes 131072 | tf_op jit(solution)/shard_map/all_to_all | solution.py:137
  75.9 1.0 fusion.38
  78.3 4.4 %all-to-all-done = bf16[8,8,512]{2,1,0:T(8,128)(2,1)S(1)} async-done(((bf16[8,8,512]{2,1,0:T(8,128)(2,1)}), bf16[8,8,512]{2,1,0:T(8,128)(2,1)S(1)}, u32[]{:S(2)}, u32[]{:S(2)}) %all-to-all-start) | async-done | bytes 65568 | tf_op jit(solution)/shard_map/all_to_all | solution.py:137
  82.7 5.8 %all_gather.7 = bf16[4,8,4096]{2,1,0:T(8,128)(2,1)S(1)} all-gather(bf16[1,8,4096]{2,1,0:T(8,128)(2,1)S(1)} %bitcast.169), channel_id=1, replica_groups=mesh['dp'=4,'expert'=8] {'dp'}, dimensions={0}, use_global_device_ids=true | all-gather | bytes 327680 | tf_op jit(solution)/shard_map/all_gather | solution.py:136
  88.5 11.8 %fusion.4 = f32[4,8,3584]{2,1,0:T(8,128)S(1)} fusion(bf16[4,8,4096]{2,1,0:T(8,128)(2,1)S(1)} %all_gather.7, bf16[1,4096,3584]{2,1,0:T(8,128)(2,1)} %param.26), kind=kOutput, calls=%fused_computation.4 | convolution fusion | flops 939524096 | bytes 30081024 | tf_op jit(solution)/shard_map/...d,df->...f/dot_general | solution.py:142
  100.3 22.4 %fusion = f32[4,8,4096]{2,1,0:T(8,128)} fusion(bf16[1,3584,4096]{2,1,0:T(8,128)(2,1)} %param.28, bf16[4,8,4096]{2,1,0:T(8,128)(2,1)S(1)} %all_gather.7, bf16[1,4096,3584]{2,1,0:T(8,128)(2,1)} %param.27, f32[4,8,3584]{2,1,0:T(8,128)S(1)} %fusion.4), kind=kOutput, calls=%fused_computation | convolution fusion | flops 1879736320 | bytes 59965440 | tf_op jit(solution)/shard_map/...f,fd->...d/dot_general | solution.py:148
  123.4 18.6 %all-reduce = (f32[2,8,8]{2,1,0:T(8,128)S(1)}, f32[2,1,128]{2,1,0:T(1,128)S(1)}) all-reduce(f32[2,8,8]{2,1,0:T(8,128)S(1)} %fusion.38, f32[2,1,128]{2,1,0:T(1,128)S(1)} %compare_select_fusion), channel_id=1, replica_groups=mesh['dp'=4,'expert'=8] {'expert'}, use_global_device_ids=true, to_apply=%region_6.7 | all-reduce | flops 384 | bytes 3072 | tf_op jit(solution)/shard_map/psum | solution.py:116
  142.4 4.8 %copy.114 = f32[1,8,4096]{1,0,2:T(1,128)} copy(f32[1,8,4096]{2,1,0:T(8,128)} %reduce-scatter.2.cloned.1.call-done) | data formatting | bytes 262144 | tf_op jit(solution)/shard_map/reduce_scatter | solution.py:147
  147.7 20.4 %reduce.7 = f32[4096,8]{1,0:T(8,128)} reduce(f32[4096,1,8]{2,1,0:T(1,128)} %bitcast.164, f32[]{:T(128)} %broadcast.178), dimensions={1}, to_apply=%bitcast.149.reduce_sub_computation | reduce | bytes 262148
  168.0 3.3 %reshape.320 = f32[8,1,4096]{2,1,0:T(1,128)} reshape(f32[4096,8]{1,0:T(8,128)} %reduce.7) | data formatting | bytes 262144
  171.3 5.1 %all-to-all-start.1 = ((f32[8,1,4096]{2,1,0:T(1,128)}), f32[8,1,4096]{2,1,0:T(1,128)S(1)}, u32[]{:S(2)}, u32[]{:S(2)}) async-start(f32[8,1,4096]{2,1,0:T(1,128)} %reshape.320), calls=%async_computation.2 | async-start | bytes 262144 | tf_op jit(solution)/shard_map/all_to_all | solution.py:153
  177.4 6.5 %all-to-all-done.1 = f32[8,1,4096]{2,1,0:T(1,128)S(1)} async-done(((f32[8,1,4096]{2,1,0:T(1,128)}), f32[8,1,4096]{2,1,0:T(1,128)S(1)}, u32[]{:S(2)}, u32[]{:S(2)}) %all-to-all-start.1) | async-done | bytes 131104 | tf_op jit(solution)/shard_map/all_to_all | solution.py:153
  183.8 1.0 reduce.8
  184.8 4.9 %reshape.321 = f32[4096,1,8]{2,1,0:T(1,128)} reshape(f32[8,4096]{1,0:T(8,128)S(1)} %reduce.8) | data formatting | bytes 262144
  189.6 2.2 %copy.131 = f32[1,8,8,512]{3,2,1,0:T(8,128)S(1)} copy(f32[1,8,8,512]{1,3,2,0:T(8,128)} %bitcast.165) | data formatting | bytes 262144 | tf_op jit(solution)/shard_map/all_to_all | solution.py:153
  (50 shorter events, 8.8 us)
Async XLA Ops:
  7.2 39.1 %copy-start = (bf16[2048,512]{1,0:T(8,128)(2,1)S(1)}, bf16[2048,512]{1,0:T(8,128)(2,1)}, u32[]{:S(2)}) copy-start(bf16[2048,512]{1,0:T(8,128)(2,1)} %param.22) | copy-start | bytes 6291460
  72.5 10.2 %all-to-all-start = ((bf16[8,8,512]{2,1,0:T(8,128)(2,1)}), bf16[8,8,512]{2,1,0:T(8,128)(2,1)S(1)}, u32[]{:S(2)}, u32[]{:S(2)}) async-start(bf16[8,8,512]{2,1,0:T(8,128)(2,1)} %copy.113), calls=%async_computation | async-start | bytes 131072 | tf_op jit(solution)/shard_map/all_to_all | solution.py:137
  75.9 66.5 %reduce-scatter.2.cloned.1.call-start = ((), (), s32[]{:S(2)}) async-start(), calls=%async_computation.3 | async-start | bytes 655360 | tf_op jit(solution)/shard_map/reduce_scatter | solution.py:147
  100.3 91.7 %copy-start.1 = (bf16[2,1,8,512]{3,2,1,0:T(8,128)(2,1)S(1)}, bf16[2,1,8,512]{3,2,1,0:T(8,128)(2,1)}, u32[]{:S(2)}) copy-start(bf16[2,1,8,512]{3,2,1,0:T(8,128)(2,1)} %param.23) | copy-start | bytes 49156
  171.3 12.5 %all-to-all-start.1 = ((f32[8,1,4096]{2,1,0:T(1,128)}), f32[8,1,4096]{2,1,0:T(1,128)S(1)}, u32[]{:S(2)}, u32[]{:S(2)}) async-start(f32[8,1,4096]{2,1,0:T(1,128)} %reshape.320), calls=%async_computation.2 | async-start | bytes 262144 | tf_op jit(solution)/shard_map/all_to_all | solution.py:153
Sparse Core Ops, SparseCore 0:
  122.9 19.1 reduce-scatter.1
where the time goes:
time: 201 us; the launch traced here: 200 us
  blocking collectives  78 us (39%)
  matrix products  40.6 us (20%)
  other arithmetic  25.3 us (13%)
  local copies, waits for them, and re-layouts  21.5 us (11%)
  between operations  14.8 us (7%)
  waiting for transfers between devices  10.9 us (5%)
  starting transfers between devices  8.52 us (4%)
    all_gather x1, blocking collectives, on_device(): lax.all_gather(attended, 'expert', axis=2, tiled=True)  32.4 us
    dot_general x1, matrix products, on_device(): jnp.einsum('...f,fd->...d', hidden, expert_down[0], preferred_element_typ...  22.4 us
    psum x1, blocking collectives, on_device(): squares_all = lax.psum(squares, 'expert')  21.3 us
    unnamed x1, other arithmetic  20.4 us
    psum x1, blocking collectives, on_device(): logits = lax.psum(partial_logits, 'expert')  18.6 us
    dot_general x1, matrix products, on_device(): jnp.einsum('...d,df->...f', tokens, expert_gate[0], preferred_element_typ...  11.8 us
    unnamed x7, local copies, waits for them, and re-layouts  8.7 us
    all_to_all x1, waiting for transfers between devices, on_device(): lax.all_to_all(partial_out, 'expert', split_axis=2, concat_axis=0, tiled=...  6.46 us
  transfers between devices with their start and end apart: 3, of which 2 were waited for; matrix products, arithmetic and copies ran while one was open for 2% of the time, Pallas kernels for 0%

commit v1 on v0

--- a/solution.py
+++ b/solution.py
@@ -12,6 +12,30 @@
 STEPS = 2
 ANSWERS = 128
 EPSILON = 1e-05
+
+
+def work_both_ways(shard, axis, dim, work, out_dim):
+    count, index, rows = (lax.axis_size(axis), lax.axis_index(axis), shard.shape[dim])
+    right = [(i, (i + 1) % count) for i in range(count)]
+    left = [(b, a) for a, b in right]
+    lower, upper = (lax.ppermute(shard, axis, right), lax.ppermute(shard, axis, left))
+    made = work(shard, index * rows)
+    length = made.shape[out_dim]
+    out = jnp.zeros((*made.shape[:out_dim], count * length, *made.shape[out_dim + 1 :]), made.dtype)
+
+    def put(out, made, source):
+        return lax.dynamic_update_slice_in_dim(out, made, source * length, axis=out_dim)
+
+    out = put(out, made, index)
+    for step in range(1, count // 2 + 1):
+        below, above = ((index - step) % count, (index + step) % count)
+        held = (lower, upper)
+        if step < count // 2:
+            lower, upper = (lax.ppermute(lower, axis, right), lax.ppermute(upper, axis, left))
+        out = put(out, work(held[0], below * rows), below)
+        if 2 * step < count:
+            out = put(out, work(held[1], above * rows), above)
+    return out
 
 
 def attend(query, keys, values, fresh_keys, fresh_values, lengths):
@@ -100,11 +124,14 @@
         cache_len.reshape(seq_count),
     ).reshape(STEPS, prompt_dev, local_count, QH * HD)
     active = (1 - stop_mask).astype(jnp.float32)
-    attn_proj = jnp.einsum(
-        "tpsq,qc->tpsc",
-        lax.all_gather(attended, "expert", axis=2, tiled=True),
-        o_proj,
-        preferred_element_type=jnp.float32,
+    attn_proj = work_both_ways(
+        attended,
+        "expert",
+        2,
+        lambda part, offset: jnp.einsum(
+            "tpsq,qc->tpsc", part, o_proj, preferred_element_type=jnp.float32
+        ),
+        2,
     )
     mixed_rows = residual_in.astype(jnp.float32) + attn_proj
     squares = jnp.sum(mixed_rows * mixed_rows, -1)

time: 201 us -> 186 us (0.925)
  blocking collectives: 78 us -> 41.7 us
  starting transfers between devices: 8.52 us -> 24.9 us
  waiting for transfers between devices: 10.9 us -> 21.2 us
  other arithmetic: 25.3 us -> 22.5 us
  local copies, waits for them, and re-layouts: 21.5 us -> 19.2 us
    all_gather x1 -> x0, blocking collectives: 32.4 us -> none  [on_device(): lax.all_gather(attended, 'expert', axis=2, tiled=True)]
    ppermute x0 -> x7, starting transfers between devices: none -> 15.9 us  [the longest x2 9.76 us: work_both_ways(): lax.ppermute(upper, axis, left)]
    ppermute x0 -> x7, waiting for transfers between devices: none -> 7.74 us  [the longest x3 7.45 us: work_both_ways(): lax.ppermute(lower, axis, right)]
    psum x1, blocking collectives: 21.3 us -> 17.1 us  [on_device(): squares_all = lax.psum(squares, 'expert')]
    all_to_all x1, waiting for transfers between devices: 4.42 us -> 6.71 us  [on_device(): lax.all_to_all(outgoing, 'expert', split_axis=0, concat_axis=2, tiled=True)]
    unnamed x7 -> x23, local copies, waits for them, and re-layouts: 8.7 us -> 8.75 us
  transfers between devices with their start and end apart: 3 -> 10, of which waited for: 2 -> 8; matrix products, arithmetic and copies ran while one was open for 2% -> 3% of each run, Pallas kernels for 0% -> 0%
where the time goes in v1:
time: 186 us; the launch traced here: 185 us
  blocking collectives  41.7 us (22%)
  matrix products  40.2 us (22%)
  starting transfers between devices  24.9 us (13%)
  other arithmetic  22.5 us (12%)
  waiting for transfers between devices  21.2 us (11%)
  local copies, waits for them, and re-layouts  19.2 us (10%)
  between operations  15.2 us (8%)
    dot_general x1, matrix products, on_device(): jnp.einsum('...f,fd->...d', hidden, expert_down[0], preferred_element_typ...  22.4 us
    unnamed x1, other arithmetic  19.4 us
    psum x1, blocking collectives, on_device(): logits = lax.psum(partial_logits, 'expert')  18.6 us
    psum x1, blocking collectives, on_device(): squares_all = lax.psum(squares, 'expert')  17.1 us
    dot_general x1, matrix products, on_device(): jnp.einsum('...d,df->...f', tokens, expert_gate[0], preferred_element_typ...  11.8 us
    ppermute x2, starting transfers between devices, work_both_ways(): lax.ppermute(upper, axis, left)  9.76 us
    unnamed x23, local copies, waits for them, and re-layouts  8.75 us
    ppermute x3, waiting for transfers between devices, work_both_ways(): lax.ppermute(lower, axis, right)  7.45 us
  transfers between devices with their start and end apart: 10, of which 8 were waited for; matrix products, arithmetic and copies ran while one was open for 3% of the time, Pallas kernels for 0%

profile of v1, /device:TPU:0, one launch (start us, length us, event | category | flops | bytes accessed | tf_op | source)
XLA Modules:
  0.0 184.8 jit_solution(10619740759047205360)
XLA Ops:
  7.2 0.9 reshape.325
  8.1 1.2 reshape.324
  10.0 0.9 convolution_multiply_fusion.1
  12.3 3.0 %collective-permute-start = (bf16[2,1,1,2048]{3,0,2,1:T(2,128)(2,1)S(1)}, bf16[2,1,1,2048]{3,0,2,1:T(2,128)(2,1)S(1)}, u32[]{:S(2)}, u32[]{:S(2)}) collective-permute-start(bf16[2,1,1,2048]{3,0,2,1:T(2,128)(2,1)S(1)} %convert_element_type.81), channel_id=1, source_target_pairs={{0,1},{1,2},{2,3},{3,4},{4,5},{5,6},{6,7},{7,0},{8,9},{9,10},{10,1... | collective-permute-start | bytes 24584 | tf_op jit(solution)/shard_map/ppermute | solution.py:21
  15.3 3.1 %collective-permute-start.1 = (bf16[2,1,1,2048]{3,0,2,1:T(2,128)(2,1)S(1)}, bf16[2,1,1,2048]{3,0,2,1:T(2,128)(2,1)S(1)}, u32[]{:S(2)}, u32[]{:S(2)}) collective-permute-start(bf16[2,1,1,2048]{3,0,2,1:T(2,128)(2,1)S(1)} %convert_element_type.81), channel_id=1, source_target_pairs={{1,0},{2,1},{3,2},{4,3},{5,4},{6,5},{7,6},{0,7},{9,8},{10,9},{11,1... | collective-permute-start | bytes 24584 | tf_op jit(solution)/shard_map/ppermute | solution.py:21
  20.9 4.8 %collective-permute-start.3 = (bf16[2,1,1,2048]{3,0,2,1:T(2,128)(2,1)S(1)}, bf16[2,1,1,2048]{3,0,2,1:T(2,128)(2,1)S(1)}, u32[]{:S(2)}, u32[]{:S(2)}) collective-permute-start(bf16[2,1,1,2048]{3,0,2,1:T(2,128)(2,1)S(1)} %collective-permute-done.1), channel_id=1, source_target_pairs={{1,0},{2,1},{3,2},{4,3},{5,4},{6,5},{7,6},{0,7},{9,8},{10,9},{11,1... | collective-permute-start | bytes 24584 | tf_op jit(solution)/shard_map/ppermute | solution.py:34
  25.7 1.0 collective-permute-done.2
  27.7 5.0 %collective-permute-start.5 = (bf16[2,1,1,2048]{3,0,2,1:T(2,128)(2,1)S(1)}, bf16[2,1,1,2048]{3,0,2,1:T(2,128)(2,1)S(1)}, u32[]{:S(2)}, u32[]{:S(2)}) collective-permute-start(bf16[2,1,1,2048]{3,0,2,1:T(2,128)(2,1)S(1)} %collective-permute-done.3), channel_id=1, source_target_pairs={{1,0},{2,1},{3,2},{4,3},{5,4},{6,5},{7,6},{0,7},{9,8},{10,9},{11,1... | collective-permute-start | bytes 24584 | tf_op jit(solution)/shard_map/ppermute | solution.py:34
  34.6 5.6 %collective-permute-done.6 = bf16[2,1,1,2048]{3,0,2,1:T(2,128)(2,1)S(1)} collective-permute-done((bf16[2,1,1,2048]{3,0,2,1:T(2,128)(2,1)S(1)}, bf16[2,1,1,2048]{3,0,2,1:T(2,128)(2,1)S(1)}, u32[]{:S(2)}, u32[]{:S(2)}) %collective-permute-start.6) | collective-permute-done | bytes 8224 | tf_op jit(solution)/shard_map/ppermute | solution.py:34
  40.7 17.1 %psum.21 = f32[2,1,8]{2,0,1:T(2,128)S(1)} all-reduce(f32[2,1,8]{2,0,1:T(2,128)S(1)} %bitcast.203), channel_id=1, replica_groups=mesh['dp'=4,'expert'=8] {'expert'}, use_global_device_ids=true, to_apply=%region_5.6 | all-reduce | flops 16 | bytes 128 | tf_op jit(solution)/shard_map/psum | solution.py:139
  58.8 3.3 %all-to-all-start = ((bf16[8,8,512]{2,1,0:T(8,128)(2,1)}), bf16[8,8,512]{2,1,0:T(8,128)(2,1)S(1)}, u32[]{:S(2)}, u32[]{:S(2)}) async-start(bf16[8,8,512]{2,1,0:T(8,128)(2,1)} %copy.150), calls=%async_computation | async-start | bytes 131072 | tf_op jit(solution)/shard_map/all_to_all | solution.py:164
  62.3 6.7 %all-to-all-done = bf16[8,8,512]{2,1,0:T(8,128)(2,1)S(1)} async-done(((bf16[8,8,512]{2,1,0:T(8,128)(2,1)}), bf16[8,8,512]{2,1,0:T(8,128)(2,1)S(1)}, u32[]{:S(2)}, u32[]{:S(2)}) %all-to-all-start) | async-done | bytes 65568 | tf_op jit(solution)/shard_map/all_to_all | solution.py:164
  69.0 6.0 %all_gather.3 = bf16[4,8,4096]{2,1,0:T(8,128)(2,1)S(1)} all-gather(bf16[1,8,4096]{2,1,0:T(8,128)(2,1)S(1)} %bitcast.200), channel_id=1, replica_groups=mesh['dp'=4,'expert'=8] {'dp'}, dimensions={0}, use_global_device_ids=true | all-gather | bytes 327680 | tf_op jit(solution)/shard_map/all_gather | solution.py:163
  74.9 11.8 %fusion.4 = f32[4,8,3584]{2,1,0:T(8,128)S(1)} fusion(bf16[4,8,4096]{2,1,0:T(8,128)(2,1)S(1)} %all_gather.3, bf16[1,4096,3584]{2,1,0:T(8,128)(2,1)} %param.26), kind=kOutput, calls=%fused_computation.4 | convolution fusion | flops 939524096 | bytes 30081024 | tf_op jit(solution)/shard_map/...d,df->...f/dot_general | solution.py:169
  86.7 22.4 %fusion = f32[4,8,4096]{2,1,0:T(8,128)} fusion(bf16[1,3584,4096]{2,1,0:T(8,128)(2,1)} %param.28, bf16[4,8,4096]{2,1,0:T(8,128)(2,1)S(1)} %all_gather.3, bf16[1,4096,3584]{2,1,0:T(8,128)(2,1)} %param.27, f32[4,8,3584]{2,1,0:T(8,128)S(1)} %fusion.4), kind=kOutput, calls=%fused_computation | convolution fusion | flops 1879736320 | bytes 59965440 | tf_op jit(solution)/shard_map/...f,fd->...d/dot_general | solution.py:175
  109.4 18.6 %all-reduce = (f32[2,8,8]{2,1,0:T(8,128)S(1)}, f32[2,1,128]{2,1,0:T(1,128)S(1)}) all-reduce(f32[2,8,8]{2,1,0:T(8,128)S(1)} %fusion.34, f32[2,1,128]{2,1,0:T(1,128)S(1)} %compare_select_fusion), channel_id=1, replica_groups=mesh['dp'=4,'expert'=8] {'expert'}, use_global_device_ids=true, to_apply=%region_6.7 | all-reduce | flops 384 | bytes 3072 | tf_op jit(solution)/shard_map/psum | solution.py:143
  128.6 4.1 %copy.151 = f32[1,8,4096]{1,0,2:T(1,128)S(1)} copy(f32[1,8,4096]{2,1,0:T(8,128)} %reduce-scatter.2.cloned.1.call-done) | data formatting | bytes 262144 | tf_op jit(solution)/shard_map/reduce_scatter | solution.py:174
  133.3 19.4 %reduce.7 = f32[4096,8]{1,0:T(8,128)} reduce(f32[4096,1,8]{2,1,0:T(1,128)S(1)} %bitcast.195, f32[]{:T(128)} %broadcast.184), dimensions={1}, to_apply=%bitcast.175.reduce_sub_computation | reduce | bytes 262148
  152.6 3.3 %reshape.355 = f32[8,1,4096]{2,1,0:T(1,128)} reshape(f32[4096,8]{1,0:T(8,128)} %reduce.7) | data formatting | bytes 262144
  156.0 5.6 %all-to-all-start.1 = ((f32[8,1,4096]{2,1,0:T(1,128)}), f32[8,1,4096]{2,1,0:T(1,128)S(1)}, u32[]{:S(2)}, u32[]{:S(2)}) async-start(f32[8,1,4096]{2,1,0:T(1,128)} %reshape.355), calls=%async_computation.2 | async-start | bytes 262144 | tf_op jit(solution)/shard_map/all_to_all | solution.py:180
  162.4 6.5 %all-to-all-done.1 = f32[8,1,4096]{2,1,0:T(1,128)S(1)} async-done(((f32[8,1,4096]{2,1,0:T(1,128)}), f32[8,1,4096]{2,1,0:T(1,128)S(1)}, u32[]{:S(2)}, u32[]{:S(2)}) %all-to-all-start.1) | async-done | bytes 131104 | tf_op jit(solution)/shard_map/all_to_all | solution.py:180
  168.9 1.1 reduce.8
  170.0 4.9 %reshape.356 = f32[4096,1,8]{2,1,0:T(1,128)} reshape(f32[8,4096]{1,0:T(8,128)S(1)} %reduce.8) | data formatting | bytes 262144
  174.8 2.2 %copy.168 = f32[1,8,8,512]{3,2,1,0:T(8,128)S(1)} copy(f32[1,8,8,512]{1,3,2,0:T(8,128)} %bitcast.196) | data formatting | bytes 262144 | tf_op jit(solution)/shard_map/all_to_all | solution.py:180
  (105 shorter events, 11.2 us)
Async XLA Ops:
  7.2 12.0 %copy-start = (bf16[2048,512]{1,0:T(8,128)(2,1)S(1)}, bf16[2048,512]{1,0:T(8,128)(2,1)}, u32[]{:S(2)}) copy-start(bf16[2048,512]{1,0:T(8,128)(2,1)} %param.22) | copy-start | bytes 6291460
  7.2 4.5 %copy-start.2 = (bf16[1,1,512,512]{3,2,1,0:T(8,128)(2,1)S(1)}, bf16[1,1,512,512]{3,2,1,0:T(8,128)(2,1)}, u32[]{:S(2)}) copy-start(bf16[1,1,512,512]{3,2,1,0:T(8,128)(2,1)} %param.18) | copy-start | bytes 1572868
  8.1 4.0 %copy-start.8 = (bf16[2,1,1,512]{3,0,2,1:T(2,128)(2,1)S(1)}, bf16[2,1,1,512]{3,0,2,1:T(2,128)(2,1)}, u32[]{:S(2)}) copy-start(bf16[2,1,1,512]{3,0,2,1:T(2,128)(2,1)} %param.20) | copy-start | bytes 6148
  8.1 10.4 %copy-start.6 = (s32[2,4,8,2]{2,3,1,0:T(2,128)S(1)}, s32[2,4,8,2]{2,3,1,0:T(2,128)}, u32[]{:S(2)}) copy-start(s32[2,4,8,2]{2,3,1,0:T(2,128)} %param.29) | copy-start | bytes 1540
  8.1 11.0 %copy-start.9 = (s32[2,1]{0,1:T(1,128)S(1)}, s32[2,1]{0,1:T(1,128)}, u32[]{:S(2)}) copy-start(s32[2,1]{0,1:T(1,128)} %param.31) | copy-start | bytes 28
  12.3 7.7 %collective-permute-start = (bf16[2,1,1,2048]{3,0,2,1:T(2,128)(2,1)S(1)}, bf16[2,1,1,2048]{3,0,2,1:T(2,128)(2,1)S(1)}, u32[]{:S(2)}, u32[]{:S(2)}) collective-permute-start(bf16[2,1,1,2048]{3,0,2,1:T(2,128)(2,1)S(1)} %convert_element_type.81), channel_id=1, source_target_pairs={{0,1},{1,2},{2,3},{3,4},{4,5},{5,6},{6,7},{7,0},{8,9},{9,10},{10,1... | collective-permute-start | bytes 24584 | tf_op jit(solution)/shard_map/ppermute | solution.py:21
  15.3 5.0 %collective-permute-start.1 = (bf16[2,1,1,2048]{3,0,2,1:T(2,128)(2,1)S(1)}, bf16[2,1,1,2048]{3,0,2,1:T(2,128)(2,1)S(1)}, u32[]{:S(2)}, u32[]{:S(2)}) collective-permute-start(bf16[2,1,1,2048]{3,0,2,1:T(2,128)(2,1)S(1)} %convert_element_type.81), channel_id=1, source_target_pairs={{1,0},{2,1},{3,2},{4,3},{5,4},{6,5},{7,6},{0,7},{9,8},{10,9},{11,1... | collective-permute-start | bytes 24584 | tf_op jit(solution)/shard_map/ppermute | solution.py:21
  20.4 6.4 %collective-permute-start.2 = (bf16[2,1,1,2048]{3,0,2,1:T(2,128)(2,1)S(1)}, bf16[2,1,1,2048]{3,0,2,1:T(2,128)(2,1)S(1)}, u32[]{:S(2)}, u32[]{:S(2)}) collective-permute-start(bf16[2,1,1,2048]{3,0,2,1:T(2,128)(2,1)S(1)} %collective-permute-done), channel_id=1, source_target_pairs={{0,1},{1,2},{2,3},{3,4},{4,5},{5,6},{6,7},{7,0},{8,9},{9,10},{10,1... | collective-permute-start | bytes 24584 | tf_op jit(solution)/shard_map/ppermute | solution.py:34
  20.9 6.2 %collective-permute-start.3 = (bf16[2,1,1,2048]{3,0,2,1:T(2,128)(2,1)S(1)}, bf16[2,1,1,2048]{3,0,2,1:T(2,128)(2,1)S(1)}, u32[]{:S(2)}, u32[]{:S(2)}) collective-permute-start(bf16[2,1,1,2048]{3,0,2,1:T(2,128)(2,1)S(1)} %collective-permute-done.1), channel_id=1, source_target_pairs={{1,0},{2,1},{3,2},{4,3},{5,4},{6,5},{7,6},{0,7},{9,8},{10,9},{11,1... | collective-permute-start | bytes 24584 | tf_op jit(solution)/shard_map/ppermute | solution.py:34
  27.1 6.4 %collective-permute-start.4 = (bf16[2,1,1,2048]{3,0,2,1:T(2,128)(2,1)S(1)}, bf16[2,1,1,2048]{3,0,2,1:T(2,128)(2,1)S(1)}, u32[]{:S(2)}, u32[]{:S(2)}) collective-permute-start(bf16[2,1,1,2048]{3,0,2,1:T(2,128)(2,1)S(1)} %collective-permute-done.2), channel_id=1, source_target_pairs={{0,1},{1,2},{2,3},{3,4},{4,5},{5,6},{6,7},{7,0},{8,9},{9,10},{10,1... | collective-permute-start | bytes 24584 | tf_op jit(solution)/shard_map/ppermute | solution.py:34
  27.7 6.4 %collective-permute-start.5 = (bf16[2,1,1,2048]{3,0,2,1:T(2,128)(2,1)S(1)}, bf16[2,1,1,2048]{3,0,2,1:T(2,128)(2,1)S(1)}, u32[]{:S(2)}, u32[]{:S(2)}) collective-permute-start(bf16[2,1,1,2048]{3,0,2,1:T(2,128)(2,1)S(1)} %collective-permute-done.3), channel_id=1, source_target_pairs={{1,0},{2,1},{3,2},{4,3},{5,4},{6,5},{7,6},{0,7},{9,8},{10,9},{11,1... | collective-permute-start | bytes 24584 | tf_op jit(solution)/shard_map/ppermute | solution.py:34
  33.8 6.8 %copy-start.3 = (bf16[2,1,8,512]{3,2,1,0:T(8,128)(2,1)S(1)}, bf16[2,1,8,512]{3,2,1,0:T(8,128)(2,1)}, u32[]{:S(2)}) copy-start(bf16[2,1,8,512]{3,2,1,0:T(8,128)(2,1)} %param.23) | copy-start | bytes 49156
  33.8 24.0 %copy-start.5 = (f32[512]{0:T(512)S(1)}, f32[512]{0:T(512)}, u32[]{:S(2)}) copy-start(f32[512]{0:T(512)} %param.24) | copy-start | bytes 6148
  33.8 28.4 %copy-start.7 = (s32[2,1,1]{0,2,1:T(1,128)S(1)}, s32[2,1,1]{0,2,1:T(1,128)}, u32[]{:S(2)}) copy-start(s32[2,1,1]{0,2,1:T(1,128)} %param.30) | copy-start | bytes 28
  33.8 6.4 %collective-permute-start.6 = (bf16[2,1,1,2048]{3,0,2,1:T(2,128)(2,1)S(1)}, bf16[2,1,1,2048]{3,0,2,1:T(2,128)(2,1)S(1)}, u32[]{:S(2)}, u32[]{:S(2)}) collective-permute-start(bf16[2,1,1,2048]{3,0,2,1:T(2,128)(2,1)S(1)} %collective-permute-done.4), channel_id=1, source_target_pairs={{0,1},{1,2},{2,3},{3,4},{4,5},{5,6},{6,7},{7,0},{8,9},{9,10},{10,1... | collective-permute-start | bytes 24584 | tf_op jit(solution)/shard_map/ppermute | solution.py:34
  58.8 10.2 %all-to-all-start = ((bf16[8,8,512]{2,1,0:T(8,128)(2,1)}), bf16[8,8,512]{2,1,0:T(8,128)(2,1)S(1)}, u32[]{:S(2)}, u32[]{:S(2)}) async-start(bf16[8,8,512]{2,1,0:T(8,128)(2,1)} %copy.150), calls=%async_computation | async-start | bytes 131072 | tf_op jit(solution)/shard_map/all_to_all | solution.py:164
  62.1 66.5 %reduce-scatter.2.cloned.1.call-start = ((), (), s32[]{:S(2)}) async-start(), calls=%async_computation.3 | async-start | bytes 655360 | tf_op jit(solution)/shard_map/reduce_scatter | solution.py:174
  86.7 22.5 %copy-start.4 = (f32[512,8]{0,1:T(8,128)S(1)}, f32[512,8]{0,1:T(8,128)}, u32[]{:S(2)}) copy-start(f32[512,8]{0,1:T(8,128)} %param.25) | copy-start | bytes 49156
  156.0 12.9 %all-to-all-start.1 = ((f32[8,1,4096]{2,1,0:T(1,128)}), f32[8,1,4096]{2,1,0:T(1,128)S(1)}, u32[]{:S(2)}, u32[]{:S(2)}) async-start(f32[8,1,4096]{2,1,0:T(1,128)} %reshape.355), calls=%async_computation.2 | async-start | bytes 262144 | tf_op jit(solution)/shard_map/all_to_all | solution.py:180
  168.9 9.1 %copy-start.1 = (bf16[2048,512]{1,0:T(8,128)(2,1)S(1)}, bf16[2048,512]{1,0:T(8,128)(2,1)}, u32[]{:S(2)}) copy-start(bf16[2048,512]{1,0:T(8,128)(2,1)} %param.22) | copy-start | bytes 6291460
Sparse Core Ops, SparseCore 0:
  109.3 19.2 reduce-scatter.1
